TPU v7x, 256 devices: a whole 4x4x8 slice. The times are simulated.
256 devices in a mesh: mem: 16 (over z, core), ma: 16 (over x, y).
Axes of the slice: x: 4, y: 4, z: 8, core: 2. Of those that a mesh axis runs over, the one named last changes fastest.
Arguments:
- ar_state: float32 [3, 64, 128, 2, 1280], P(None, 'mem', 'ma'), may hold values from -4 to 4
- forcing: float32 [3, 64, 128, 2, 1280], P(None, 'mem', 'ma'), may hold values from -6 to 6
- ar_decay: float32 [3], replicated, may hold values from 0.3 to 0.95
- amplitude: float32 [3, 1280], replicated, may hold values from 0.05 to 0.4
- wavenumber: int32 [128], replicated, may hold values from 0 to 1279, as said below
- tables: bfloat16 [128, 1280, 1280], P('ma', None, 'mem'), may hold values from -0.15625 to 0.15625
- tendencies: bfloat16 [64, 1280, 5120], P('mem', 'ma'), may hold values from -6 to 6
Outputs:
- perturbed: bfloat16 [64, 1280, 5120], P('mem', 'ma')
- new_state: float32 [3, 64, 128, 2, 1280], P(None, 'mem', 'ma')
Inputs may be any that keep to these rules, and one draw needn't show every extreme that they name: `wavenumber`: 128 distinct values.
All inputs are finite; a program needn't handle non-finite values.
Results may differ from a plain program's by a relative error of at most 0.0042.
Values may be sent and summed in bfloat16 or wider, within the bound.
No kernel may reach another device: no remote copies, remote signals or barrier semaphores. Data moves between devices by JAX's collectives and lax.ppermute only.
A program may use at most 64 MiB of HBM per device.

v0:
```python
import math
import jax
import jax.numpy as jnp
from jax import lax
from jax.sharding import PartitionSpec as P

clip_level = 0.9


def basis_table(wavenumber, lon_count):
    longitude = lax.broadcasted_iota(jnp.int32, (wavenumber.shape[0], lon_count), 1)
    phases = wavenumber[:, None] * longitude % lon_count
    angles = phases.astype(jnp.float32) * (2.0 * math.pi / lon_count)
    stacked = jnp.stack([jnp.cos(angles), -jnp.sin(angles)], axis=1)
    return stacked.reshape(2 * wavenumber.shape[0], lon_count).astype(jnp.bfloat16)


def per_device(ar_state, forcing, ar_decay, amplitude, wavenumber, tables, tendencies):
    local_waves = ar_state.shape[2]
    degree_count = ar_state.shape[4]
    owner_index = lax.axis_index("ma")
    own_waves = lax.dynamic_slice_in_dim(wavenumber, owner_index * local_waves, local_waves)
    degree_grid = lax.broadcasted_iota(jnp.int32, (local_waves, degree_count), 1)
    kept_mask = (degree_grid >= own_waves[:, None]).astype(jnp.float32)
    updated = (
        ar_decay[:, None, None, None, None] * ar_state + amplitude[:, None, None, None, :] * forcing
    )
    new_state = kept_mask[None, None, :, None, :] * updated
    coefficients = jnp.sum(new_state, axis=0).astype(jnp.bfloat16)
    everyone = lax.all_gather(coefficients, "mem", axis=0, tiled=True)
    product = jnp.einsum("bmcn,mnl->blmc", everyone, tables, preferred_element_type=jnp.float32)
    fourier = product.astype(jnp.bfloat16)
    banded = lax.all_to_all(
        lax.all_to_all(fourier, "mem", split_axis=0, concat_axis=1, tiled=True),
        "ma",
        split_axis=1,
        concat_axis=2,
        tiled=True,
    )
    member_count, lat_rows, window_size, reim_parts = banded.shape
    basis = basis_table(wavenumber, tendencies.shape[2])
    fourier_rows = banded.reshape(member_count * lat_rows, window_size * reim_parts)
    pattern = jnp.dot(fourier_rows, basis, preferred_element_type=jnp.float32) * (
        1.0 / math.sqrt(window_size)
    )
    pattern = jnp.clip(pattern, -clip_level, clip_level).reshape(tendencies.shape)
    perturbed = (tendencies.astype(jnp.float32) * (1.0 + pattern)).astype(jnp.bfloat16)
    return (perturbed, new_state)


def solution(mesh):
    return jax.shard_map(
        per_device,
        mesh=mesh,
        in_specs=(
            P(None, "mem", "ma", None, None),
            P(None, "mem", "ma", None, None),
            P(),
            P(),
            P(),
            P("ma", None, "mem"),
            P("mem", "ma", None),
        ),
        out_specs=(P("mem", "ma", None), P(None, "mem", "ma", None, None)),
        check_vma=False,
    )
```

profile of v0, /device:TPU:1, one launch (start us, length us, event | category | flops | bytes accessed | tf_op | source)
XLA Modules:
  0.0 131.1 jit_solution(6090136942241296516)
XLA Ops:
  7.2 0.0 copy-start
  7.2 0.0 all-gather.2.cloned.1.call-start
  7.2 0.8 dynamic_slice.3
  8.1 0.1 fusion.20
  8.1 3.5 %fusion.21 = (bf16[4,8,2,1280]{3,2,1,0:T(2,128)(2,1)S(1)}, f32[3,4,8,2,1280]{4,3,2,1,0:T(2,128)}) fusion(f32[3,4,8,2,1280]{4,3,2,1,0:T(2,128)} %param.8, f32[3,1280]{1,0:T(4,128)} %param.10, f32[3,4,8,2,1280]{4,3,2,1,0:T(2,128)} %param.7, f32[3]{0:T(128)} %param.9, f32[8,1280]{1,0:T(8,128)S(1)} %fusion.20), kind=kLoop, calls=%fused_computation.23 | loop fusion | flops 1146880 | bytes 3169292 | tf_op jit(solution)/shard_map/reduce_sum | solution.py:29
  11.6 0.7 copy.23
  12.3 0.0 all-gather.2.cloned.1.call-update
  12.3 0.0 copy-start.2
  12.3 44.4 %all-gather.2.cloned.1.call-done = bf16[64,8,2,1280]{3,1,2,0:T(8,128)(2,1)} async-done(((bf16[4,8,2,1280]{3,1,2,0:T(8,128)(2,1)}), bf16[64,8,2,1280]{3,1,2,0:T(8,128)(2,1)}) %all-gather.2.cloned.1.call-update) | async-done | bytes 2621456 | tf_op jit(solution)/shard_map/all_gather | solution.py:30
  56.7 0.0 copy-done
  56.7 2.7 %fusion.15 = bf16[64,80,8,2]{1,0,3,2:T(8,128)(2,1)S(1)} fusion(bf16[8,1280,80]{1,2,0:T(8,128)(2,1)S(1)} %copy-done, bf16[64,8,2,1280]{3,1,2,0:T(8,128)(2,1)} %all-gather.2.cloned.1.call-done), kind=kOutput, calls=%fused_computation.18 | convolution fusion | flops 209797120 | bytes 4423680 | tf_op jit(solution)/shard_map/bmcn,mnl->blmc/dot_general | solution.py:31
  59.4 1.0 copy.25
  60.4 4.6 %all-to-all-start = ((bf16[64,80,8,2]{1,3,2,0:T(2,128)(2,1)}), bf16[64,80,8,2]{1,3,2,0:T(2,128)(2,1)S(1)}, u32[]{:S(2)}, u32[]{:S(2)}) async-start(bf16[64,80,8,2]{1,3,2,0:T(2,128)(2,1)} %copy.25), calls=%async_computation | async-start | bytes 524288 | tf_op jit(solution)/shard_map/all_to_all | solution.py:34
  65.0 0.0 copy-done.2
  65.0 12.1 %cosine_convert_fusion = (bf16[128,1,5120]{2,0,1:T(8,128)(2,1)S(1)}, bf16[128,1,5120]{2,0,1:T(8,128)(2,1)}) fusion(s32[128]{0:T(128)S(1)} %copy-done.2), kind=kLoop, calls=%fused_computation.11 | loop fusion | flops 7864320 | bytes 2621952 | tf_op jit(solution)/shard_map/convert
  77.1 0.0 all-to-all-done
  77.1 0.2 copy.39
  77.3 4.0 %copy.31 = bf16[4,16,80,8,2]{3,4,0,2,1:T(2,128)(2,1)} copy(bf16[4,16,80,8,2]{2,1,3,4,0:T(8,128)(2,1)S(1)} %bitcast.30) | data formatting | bytes 327680 | tf_op jit(solution)/shard_map/all_to_all | solution.py:34
  81.2 8.6 %reshape.114 = bf16[16,2,2560]{2,1,0:T(2,128)(2,1)} reshape(bf16[1280,4,2,8]{3,2,1,0:T(2,128)(2,1)} %bitcast.26) | data formatting | bytes 327680
  89.8 6.5 %all-to-all-start.1 = ((bf16[16,2,2560]{2,1,0:T(2,128)(2,1)}), bf16[16,2,2560]{2,1,0:T(2,128)(2,1)S(1)}, u32[]{:S(2)}, u32[]{:S(2)}) async-start(bf16[16,2,2560]{2,1,0:T(2,128)(2,1)} %reshape.114), calls=%async_computation.1 | async-start | bytes 327680 | tf_op jit(solution)/shard_map/all_to_all | solution.py:33
  96.4 1.6 %pad_maximum_fusion = bf16[128,2,5120]{2,0,1:T(8,128)(2,1)S(1)} fusion(bf16[128,1,5120]{2,0,1:T(8,128)(2,1)} %get-tuple-element.5, bf16[128,1,5120]{2,0,1:T(8,128)(2,1)S(1)} %get-tuple-element.4), kind=kLoop, calls=%fused_computation.7 | loop fusion | flops 1310720 | bytes 5242880 | tf_op jit(solution)/shard_map/stack | solution.py:14
  97.9 4.2 %copy.29 = bf16[128,2,5120]{2,1,0:T(2,128)(2,1)} copy(bf16[128,2,5120]{2,0,1:T(8,128)(2,1)S(1)} %pad_maximum_fusion) | data formatting | bytes 5242880 | tf_op jit(solution)/shard_map/stack | solution.py:14
  102.1 6.5 %convert_element_type.52 = bf16[256,5120]{1,0:T(8,128)(2,1)} reshape(bf16[128,2,5120]{2,1,0:T(2,128)(2,1)} %copy.29) | data formatting | bytes 5242880 | tf_op jit(solution)/shard_map/convert_element_type | solution.py:15
  108.6 0.0 all-to-all-done.1
  108.6 4.1 %reshape.115 = bf16[1280,4,2,8]{3,2,1,0:T(2,128)(2,1)} reshape(bf16[16,2,2560]{2,1,0:T(2,128)(2,1)S(1)} %all-to-all-done.1) | data formatting | bytes 327680
  112.7 5.2 %copy.28 = bf16[4,16,80,8,2]{2,0,4,3,1:T(4,128)(2,1)S(1)} copy(bf16[4,16,80,8,2]{3,4,0,2,1:T(2,128)(2,1)} %bitcast.27) | data formatting | bytes 327680 | tf_op jit(solution)/shard_map/all_to_all | solution.py:33
  117.9 0.2 reshape.112
  118.1 0.0 copy-start.1
  118.1 3.4 %fusion.1 = f32[320,5120]{1,0:T(8,128)S(1)} fusion(bf16[320,256]{0,1:T(8,128)(2,1)S(1)} %reshape.112, bf16[256,5120]{1,0:T(8,128)(2,1)} %convert_element_type.52), kind=kOutput, calls=%fused_computation.2 | convolution fusion | flops 843776000 | bytes 9338880 | tf_op jit(solution)/shard_map/dot_general | solution.py:43
  121.6 0.0 copy-done.1
  121.6 2.7 %multiply_convert_fusion = bf16[4,80,5120]{2,1,0:T(8,128)(2,1)} fusion(f32[4,80,5120]{2,1,0:T(8,128)S(1)} %bitcast.25, bf16[4,80,5120]{2,1,0:T(8,128)(2,1)S(1)} %copy-done.1), kind=kLoop, calls=%fused_computation.3 | loop fusion | flops 4915200 | bytes 13107200 | tf_op jit(solution)/shard_map/convert_element_type | solution.py:47
Async XLA Ops:
  7.2 49.6 %copy-start = (bf16[8,1280,80]{1,2,0:T(8,128)(2,1)S(1)}, bf16[8,1280,80]{1,2,0:T(8,128)(2,1)}, u32[]{:S(2)}) copy-start(bf16[8,1280,80]{1,2,0:T(8,128)(2,1)} %param.12) | copy-start | bytes 4915204
  7.2 49.6 %all-gather.2.cloned.1.call-start = ((), (), s32[]{:S(2)}) async-start(), calls=%async_computation.2 | async-start | bytes 2785280 | tf_op jit(solution)/shard_map/all_gather | solution.py:30
  12.3 52.7 %copy-start.2 = (s32[128]{0:T(128)S(1)}, s32[128]{0:T(128)}, u32[]{:S(2)}) copy-start(s32[128]{0:T(128)} %param.11) | copy-start | bytes 1540
  60.4 16.7 %all-to-all-start = ((bf16[64,80,8,2]{1,3,2,0:T(2,128)(2,1)}), bf16[64,80,8,2]{1,3,2,0:T(2,128)(2,1)S(1)}, u32[]{:S(2)}, u32[]{:S(2)}) async-start(bf16[64,80,8,2]{1,3,2,0:T(2,128)(2,1)} %copy.25), calls=%async_computation | async-start | bytes 524288 | tf_op jit(solution)/shard_map/all_to_all | solution.py:34
  89.8 18.8 %all-to-all-start.1 = ((bf16[16,2,2560]{2,1,0:T(2,128)(2,1)}), bf16[16,2,2560]{2,1,0:T(2,128)(2,1)S(1)}, u32[]{:S(2)}, u32[]{:S(2)}) async-start(bf16[16,2,2560]{2,1,0:T(2,128)(2,1)} %reshape.114), calls=%async_computation.1 | async-start | bytes 327680 | tf_op jit(solution)/shard_map/all_to_all | solution.py:33
  118.1 3.4 %copy-start.1 = (bf16[4,80,5120]{2,1,0:T(8,128)(2,1)S(1)}, bf16[4,80,5120]{2,1,0:T(8,128)(2,1)}, u32[]{:S(2)}) copy-start(bf16[4,80,5120]{2,1,0:T(8,128)(2,1)} %param.13) | copy-start | bytes 9830404
Sparse Core Ops, SparseCore 0:
  12.4 44.2 all-gather.1
where the time goes:
time: 132 us; the launch traced here: 131 us
  waiting for transfers between devices  44.4 us (34%)
  local copies, waits for them, and re-layouts  35.5 us (27%)
  other arithmetic  19.9 us (15%)
  between operations  14.1 us (11%)
  starting transfers between devices  11.2 us (8%)
  matrix products  6.1 us (5%)
    all_gather x1, waiting for transfers between devices, per_device(): everyone = lax.all_gather(coefficients, 'mem', axis=0, tiled=True)  44.4 us
    unnamed x8, local copies, waits for them, and re-layouts  12.8 us
    another operation x1, other arithmetic  12.1 us
    all_to_all x1, starting transfers between devices, per_device(): lax.all_to_all(lax.all_to_all(fourier, 'mem', split_axis=0, concat_axis=1...  6.53 us
    convert_element_type x1, local copies, waits for them, and re-layouts, basis_table(): stacked.reshape(2 * wavenumber.shape[0], lon_count).astype(jnp.bfloat16)  6.47 us
    all_to_all x1, local copies, waits for them, and re-layouts, per_device(): lax.all_to_all(lax.all_to_all(fourier, 'mem', split_axis=0, concat_axis=1...  5.18 us
    all_to_all x1, starting transfers between devices, per_device(): lax.all_to_all(fourier, 'mem', split_axis=0, concat_axis=1, tiled=True)  4.59 us
    another operation x1, local copies, waits for them, and re-layouts, basis_table(): stacked = jnp.stack([jnp.cos(angles), -jnp.sin(angles)], axis=1)  4.19 us
  transfers between devices with their start and end apart: 3, of which 1 were waited for; matrix products, arithmetic and copies ran while one was open for 19% of the time, Pallas kernels for 0%

commit v1 on v0

--- a/solution.py
+++ b/solution.py
@@ -27,7 +27,17 @@
     )
     new_state = kept_mask[None, None, :, None, :] * updated
     coefficients = jnp.sum(new_state, axis=0).astype(jnp.bfloat16)
-    everyone = lax.all_gather(coefficients, "mem", axis=0, tiled=True)
+
+    def _link_roads(ax_name, x_part):
+        block_out = jnp.concatenate(
+            lax.all_to_all(
+                jnp.stack([x_part for _ in range(lax.axis_size(ax_name))]), ax_name, 0, 0
+            ),
+            axis=0,
+        )
+        return block_out
+
+    everyone = _link_roads("mem", coefficients)
     product = jnp.einsum("bmcn,mnl->blmc", everyone, tables, preferred_element_type=jnp.float32)
     fourier = product.astype(jnp.bfloat16)
     banded = lax.all_to_all(

time: 132 us -> 153 us (1.16)
  blocking collectives: 0 us -> 71.9 us
  waiting for transfers between devices: 44.4 us -> 0.01 us
  between operations: 14.1 us -> 0.74 us
  local copies, waits for them, and re-layouts: 35.5 us -> 44 us
    all_to_all x0 -> x1, blocking collectives: none -> 71.9 us  [_link_roads(): lax.all_to_all(jnp.stack([x_part for _ in range(lax.axis_size(ax_name))])...]
    all_gather x1 -> x0, waiting for transfers between devices: 44.4 us -> none  [per_device(): everyone = lax.all_gather(coefficients, 'mem', axis=0, tiled=True)]
    reshape x0 -> x1, local copies, waits for them, and re-layouts: none -> 5.32 us  [_link_roads(): jnp.concatenate(lax.all_to_all(jnp.stack([x_part for _ in range(lax.axis_...]
    all_to_all x0 -> x1, local copies, waits for them, and re-layouts: none -> 2.76 us  [_link_roads(): lax.all_to_all(jnp.stack([x_part for _ in range(lax.axis_size(ax_name))])...]
  transfers between devices with their start and end apart: 3 -> 2, of which waited for: 1 -> 0; matrix products, arithmetic and copies ran while one was open for 19% -> 16% of each run, Pallas kernels for 0% -> 0%
where the time goes in v1:
time: 153 us
  blocking collectives  71.9 us (47%)
  local copies, waits for them, and re-layouts  44 us (29%)
  other arithmetic  19.9 us (13%)
  starting transfers between devices  10.2 us (7%)
  matrix products  5.99 us (4%)
    all_to_all x1, blocking collectives, _link_roads(): lax.all_to_all(jnp.stack([x_part for _ in range(lax.axis_size(ax_name))])...  71.9 us
    unnamed x8, local copies, waits for them, and re-layouts  12.8 us
    another operation x1, other arithmetic  12.1 us
    all_to_all x1, starting transfers between devices, per_device(): lax.all_to_all(lax.all_to_all(fourier, 'mem', split_axis=0, concat_axis=1...  6.76 us
    convert_element_type x1, local copies, waits for them, and re-layouts, basis_table(): stacked.reshape(2 * wavenumber.shape[0], lon_count).astype(jnp.bfloat16)  6.49 us
    reshape x1, local copies, waits for them, and re-layouts, _link_roads(): jnp.concatenate(lax.all_to_all(jnp.stack([x_part for _ in range(lax.axis_...  5.32 us
    all_to_all x1, local copies, waits for them, and re-layouts, per_device(): lax.all_to_all(lax.all_to_all(fourier, 'mem', split_axis=0, concat_axis=1...  5.18 us
    another operation x1, local copies, waits for them, and re-layouts, basis_table(): stacked = jnp.stack([jnp.cos(angles), -jnp.sin(angles)], axis=1)  4.19 us
  transfers between devices with their start and end apart: 2, of which 0 were waited for; matrix products, arithmetic and copies ran while one was open for 16% of the time, Pallas kernels for 0%

profile of v1, /device:TPU:1, one launch (start us, length us, event | category | flops | bytes accessed | tf_op | source)
XLA Modules:
  0.0 152.7 jit_solution(5764345547599936087)
XLA Ops:
  0.6 0.0 copy-start
  0.6 0.9 dynamic_slice.3
  1.5 0.1 fusion.15
  1.6 3.5 %fusion.16 = (bf16[4,8,2,1280]{3,2,1,0:T(2,128)(2,1)S(1)}, f32[3,4,8,2,1280]{4,3,2,1,0:T(2,128)}) fusion(f32[3,4,8,2,1280]{4,3,2,1,0:T(2,128)} %param.8, f32[3,1280]{1,0:T(4,128)} %param.10, f32[3,4,8,2,1280]{4,3,2,1,0:T(2,128)} %param.7, f32[3]{0:T(128)} %param.9, f32[8,1280]{1,0:T(8,128)S(1)} %fusion.15), kind=kLoop, calls=%fused_computation.22 | loop fusion | flops 1146880 | bytes 3169292 | tf_op jit(solution)/shard_map/reduce_sum | solution.py:29
  5.0 0.1 copy.23
  5.1 1.0 stack.5
  6.1 71.9 %all_to_all.38 = bf16[16,4,8,2,1280]{4,1,3,2,0:T(4,128)(2,1)S(1)} all-to-all(bf16[16,4,8,2,1280]{4,1,3,2,0:T(4,128)(2,1)S(1)} %stack.5), channel_id=1, replica_groups=mesh['mem'=16,'ma'=16] {'mem'}, dimensions={0} | all-to-all | bytes 5242880 | tf_op jit(solution)/shard_map/all_to_all | solution.py:33
  78.0 2.8 %copy.24 = bf16[16,4,8,2,1280]{4,1,0,3,2:T(4,128)(2,1)} copy(bf16[16,4,8,2,1280]{4,1,3,2,0:T(4,128)(2,1)S(1)} %all_to_all.38) | data formatting | bytes 5242880 | tf_op jit(solution)/shard_map/all_to_all | solution.py:33
  80.8 5.3 %reshape.117 = bf16[64,8,2,1280]{3,0,2,1:T(8,128)(2,1)} reshape(bf16[16,4,8,2,1280]{4,1,0,3,2:T(4,128)(2,1)} %copy.24) | data formatting | bytes 5242880 | tf_op jit(solution)/shard_map/reshape | solution.py:32
  86.1 0.0 copy-done
  86.1 0.0 copy-start.2
  86.1 2.6 %fusion.12 = bf16[64,80,8,2]{1,0,3,2:T(8,128)(2,1)S(1)} fusion(bf16[64,8,2,1280]{3,0,2,1:T(8,128)(2,1)} %reshape.117, bf16[8,1280,80]{1,2,0:T(8,128)(2,1)S(1)} %copy-done), kind=kOutput, calls=%fused_computation.17 | convolution fusion | flops 209797120 | bytes 4423680 | tf_op jit(solution)/shard_map/bmcn,mnl->blmc/dot_general | solution.py:41
  88.7 1.0 copy.25
  89.7 3.4 %all-to-all-start.1 = ((bf16[64,80,8,2]{1,3,2,0:T(2,128)(2,1)}), bf16[64,80,8,2]{1,3,2,0:T(2,128)(2,1)S(1)}, u32[]{:S(2)}, u32[]{:S(2)}) async-start(bf16[64,80,8,2]{1,3,2,0:T(2,128)(2,1)} %copy.25), calls=%async_computation.1 | async-start | bytes 524288 | tf_op jit(solution)/shard_map/all_to_all | solution.py:44
  93.1 0.0 copy-done.2
  93.1 12.1 %cosine_convert_fusion = (bf16[128,1,5120]{2,0,1:T(8,128)(2,1)S(1)}, bf16[128,1,5120]{2,0,1:T(8,128)(2,1)}) fusion(s32[128]{0:T(128)S(1)} %copy-done.2), kind=kLoop, calls=%fused_computation.9 | loop fusion | flops 7864320 | bytes 2621952 | tf_op jit(solution)/shard_map/convert
  105.2 0.0 all-to-all-done.1
  105.2 0.2 copy.33
  105.4 4.0 %copy.31 = bf16[4,16,80,8,2]{3,4,0,2,1:T(2,128)(2,1)} copy(bf16[4,16,80,8,2]{2,1,3,4,0:T(8,128)(2,1)S(1)} %bitcast.33) | data formatting | bytes 327680 | tf_op jit(solution)/shard_map/all_to_all | solution.py:44
  109.4 8.6 %reshape.120 = bf16[16,2,2560]{2,1,0:T(2,128)(2,1)} reshape(bf16[1280,4,2,8]{3,2,1,0:T(2,128)(2,1)} %bitcast.29) | data formatting | bytes 327680
  118.0 6.8 %all-to-all-start.2 = ((bf16[16,2,2560]{2,1,0:T(2,128)(2,1)}), bf16[16,2,2560]{2,1,0:T(2,128)(2,1)S(1)}, u32[]{:S(2)}, u32[]{:S(2)}) async-start(bf16[16,2,2560]{2,1,0:T(2,128)(2,1)} %reshape.120), calls=%async_computation.2 | async-start | bytes 327680 | tf_op jit(solution)/shard_map/all_to_all | solution.py:43
  124.8 1.6 %pad_maximum_fusion = bf16[128,2,5120]{2,0,1:T(8,128)(2,1)S(1)} fusion(bf16[128,1,5120]{2,0,1:T(8,128)(2,1)} %get-tuple-element.5, bf16[128,1,5120]{2,0,1:T(8,128)(2,1)S(1)} %get-tuple-element.4), kind=kLoop, calls=%fused_computation.7 | loop fusion | flops 1310720 | bytes 5242880 | tf_op jit(solution)/shard_map/stack | solution.py:14
  126.3 4.2 %copy.29 = bf16[128,2,5120]{2,1,0:T(2,128)(2,1)} copy(bf16[128,2,5120]{2,0,1:T(8,128)(2,1)S(1)} %pad_maximum_fusion) | data formatting | bytes 5242880 | tf_op jit(solution)/shard_map/stack | solution.py:14
  130.5 6.5 %convert_element_type.54 = bf16[256,5120]{1,0:T(8,128)(2,1)} reshape(bf16[128,2,5120]{2,1,0:T(2,128)(2,1)} %copy.29) | data formatting | bytes 5242880 | tf_op jit(solution)/shard_map/convert_element_type | solution.py:15
  137.0 0.0 all-to-all-done.2
  137.0 4.1 %reshape.121 = bf16[1280,4,2,8]{3,2,1,0:T(2,128)(2,1)} reshape(bf16[16,2,2560]{2,1,0:T(2,128)(2,1)S(1)} %all-to-all-done.2) | data formatting | bytes 327680
  141.1 5.2 %copy.28 = bf16[4,16,80,8,2]{2,0,4,3,1:T(4,128)(2,1)S(1)} copy(bf16[4,16,80,8,2]{3,4,0,2,1:T(2,128)(2,1)} %bitcast.30) | data formatting | bytes 327680 | tf_op jit(solution)/shard_map/all_to_all | solution.py:43
  146.3 0.2 reshape.118
  146.5 0.0 copy-start.1
  146.5 3.4 %fusion.1 = f32[320,5120]{1,0:T(8,128)S(1)} fusion(bf16[320,256]{0,1:T(8,128)(2,1)S(1)} %reshape.118, bf16[256,5120]{1,0:T(8,128)(2,1)} %convert_element_type.54), kind=kOutput, calls=%fused_computation.2 | convolution fusion | flops 843776000 | bytes 9338880 | tf_op jit(solution)/shard_map/dot_general | solution.py:53
  150.0 0.0 copy-done.1
  150.0 2.7 %multiply_convert_fusion = bf16[4,80,5120]{2,1,0:T(8,128)(2,1)} fusion(f32[4,80,5120]{2,1,0:T(8,128)S(1)} %bitcast.28, bf16[4,80,5120]{2,1,0:T(8,128)(2,1)S(1)} %copy-done.1), kind=kLoop, calls=%fused_computation.3 | loop fusion | flops 4915200 | bytes 13107200 | tf_op jit(solution)/shard_map/convert_element_type | solution.py:57
Async XLA Ops:
  0.6 85.5 %copy-start = (bf16[8,1280,80]{1,2,0:T(8,128)(2,1)S(1)}, bf16[8,1280,80]{1,2,0:T(8,128)(2,1)}, u32[]{:S(2)}) copy-start(bf16[8,1280,80]{1,2,0:T(8,128)(2,1)} %param.12) | copy-start | bytes 4915204
  86.1 7.0 %copy-start.2 = (s32[128]{0:T(128)S(1)}, s32[128]{0:T(128)}, u32[]{:S(2)}) copy-start(s32[128]{0:T(128)} %param.11) | copy-start | bytes 1540
  89.7 15.5 %all-to-all-start.1 = ((bf16[64,80,8,2]{1,3,2,0:T(2,128)(2,1)}), bf16[64,80,8,2]{1,3,2,0:T(2,128)(2,1)S(1)}, u32[]{:S(2)}, u32[]{:S(2)}) async-start(bf16[64,80,8,2]{1,3,2,0:T(2,128)(2,1)} %copy.25), calls=%async_computation.1 | async-start | bytes 524288 | tf_op jit(solution)/shard_map/all_to_all | solution.py:44
  118.0 19.0 %all-to-all-start.2 = ((bf16[16,2,2560]{2,1,0:T(2,128)(2,1)}), bf16[16,2,2560]{2,1,0:T(2,128)(2,1)S(1)}, u32[]{:S(2)}, u32[]{:S(2)}) async-start(bf16[16,2,2560]{2,1,0:T(2,128)(2,1)} %reshape.120), calls=%async_computation.2 | async-start | bytes 327680 | tf_op jit(solution)/shard_map/all_to_all | solution.py:43
  146.5 3.4 %copy-start.1 = (bf16[4,80,5120]{2,1,0:T(8,128)(2,1)S(1)}, bf16[4,80,5120]{2,1,0:T(8,128)(2,1)}, u32[]{:S(2)}) copy-start(bf16[4,80,5120]{2,1,0:T(8,128)(2,1)} %param.13) | copy-start | bytes 9830404
